TPU v7x, 32 devices: a whole 2x2x4 slice. The times are simulated.
32 devices in a mesh: expert: 4 (over x, core), shard: 8 (over z, y).
Axes of the slice: x: 2, y: 2, z: 4, core: 2. Of those that a mesh axis runs over, the one named last changes fastest.
Arguments:
- master_gate: float32 [64, 2048, 1024], P('expert', 'shard'), may hold values from -0.1875 to 0.1875
- second_gate: bfloat16 [64, 2048, 1024], P('expert', 'shard'), may hold values from -0.0625 to 0.0625
- master_up: float32 [64, 2048, 1024], P('expert', 'shard'), may hold values from -0.1875 to 0.1875
- second_up: bfloat16 [64, 2048, 1024], P('expert', 'shard'), may hold values from -0.0625 to 0.0625
- master_down: float32 [64, 1024, 2048], P('expert', None, 'shard'), may hold values from -0.25 to 0.25
- second_down: bfloat16 [64, 1024, 2048], P('expert', None, 'shard'), may hold values from -0.09375 to 0.09375
- router_weight: float32 [2048, 64], P('shard', 'expert'), may hold values from -0.125 to 0.125
- router_gain: float32 [2048], P('shard'), may hold values from 0.25 to 1.75
Outputs:
- final_gate: bfloat16 [64, 2048, 1024], P('expert', None, 'shard')
- final_up: bfloat16 [64, 2048, 1024], P('expert', None, 'shard')
- final_down: bfloat16 [64, 1024, 2048], P('expert', 'shard')
- scale_gate: float32 [64, 1024], P('expert', 'shard')
- scale_up: float32 [64, 1024], P('expert', 'shard')
- scale_down: float32 [64, 1024], P('expert', 'shard')
- serve_router: bfloat16 [2048, 64], replicated
All inputs are finite; a program needn't handle non-finite values. Where the computation divides by a largest or mean magnitude, that divisor is 1e-20 or more.
Results may differ from a plain program's by a relative error of at most 0.001.
Values may be sent and summed in bfloat16 or wider, within the bound.
A program may use at most 192 MiB of HBM per device.

v0:
```python
import jax
import jax.numpy as jnp
from jax import lax
from jax.sharding import PartitionSpec as P


def per_device(
    master_gate,
    second_gate,
    master_up,
    second_up,
    master_down,
    second_down,
    router_weight,
    router_gain,
):
    merged_gate = master_gate + second_gate.astype(jnp.float32)
    merged_up = master_up + second_up.astype(jnp.float32)
    merged_down = master_down + second_down.astype(jnp.float32)
    scale_gate, scale_up, scale_down = lax.pmax(
        (
            jnp.max(jnp.abs(merged_gate), axis=1),
            jnp.max(jnp.abs(merged_up), axis=1),
            jnp.max(jnp.abs(merged_down), axis=2),
        ),
        "shard",
    )
    narrow_gate, narrow_up, narrow_down = (
        (merged_gate / jnp.expand_dims(scale_gate, 1)).astype(jnp.bfloat16),
        (merged_up / jnp.expand_dims(scale_up, 1)).astype(jnp.bfloat16),
        (merged_down / jnp.expand_dims(scale_down, 2)).astype(jnp.bfloat16),
    )
    final_gate, final_up = (
        lax.all_to_all(narrow_gate, "shard", split_axis=2, concat_axis=1, tiled=True),
        lax.all_to_all(narrow_up, "shard", split_axis=2, concat_axis=1, tiled=True),
    )
    final_down = lax.all_to_all(narrow_down, "shard", split_axis=1, concat_axis=2, tiled=True)
    scale_gate = lax.dynamic_slice_in_dim(
        scale_gate, lax.axis_index("shard") * final_gate.shape[2], final_gate.shape[2], axis=1
    )
    scale_up = lax.dynamic_slice_in_dim(
        scale_up, lax.axis_index("shard") * final_up.shape[2], final_up.shape[2], axis=1
    )
    scale_down = lax.dynamic_slice_in_dim(
        scale_down, lax.axis_index("shard") * final_down.shape[1], final_down.shape[1], axis=1
    )
    part_router = (router_weight * router_gain[:, None]).astype(jnp.bfloat16)
    row_router = lax.all_gather(part_router, "shard", axis=0, tiled=True)
    serve_router = lax.all_gather(row_router, "expert", axis=1, tiled=True)
    return (final_gate, final_up, final_down, scale_gate, scale_up, scale_down, serve_router)


def solution(mesh):
    in_specs = (
        P("expert", "shard", None),
        P("expert", "shard", None),
        P("expert", "shard", None),
        P("expert", "shard", None),
        P("expert", None, "shard"),
        P("expert", None, "shard"),
        P("shard", "expert"),
        P("shard"),
    )
    out_specs = (
        P("expert", None, "shard"),
        P("expert", None, "shard"),
        P("expert", "shard", None),
        P("expert", "shard"),
        P("expert", "shard"),
        P("expert", "shard"),
        P(),
    )
    return jax.shard_map(
        per_device, mesh=mesh, in_specs=in_specs, out_specs=out_specs, check_vma=False
    )
```

profile of v0, /device:TPU:0, one launch (start us, length us, event | category | flops | bytes accessed | tf_op | source)
XLA Modules:
  0.0 877.2 jit_solution(5564650451525219035)
XLA Ops:
  7.2 17.6 %copy.34 = f32[16,256,1024]{1,0,2:T(8,128)} copy(f32[16,256,1024]{2,1,0:T(8,128)} %param.10) | data formatting | bytes 33554432 | tf_op args[2]
  24.8 12.5 %copy.33 = bf16[16,256,1024]{1,0,2:T(8,128)(2,1)} copy(bf16[16,256,1024]{2,1,0:T(8,128)(2,1)} %param.11) | data formatting | bytes 16777216 | tf_op args[3]
  37.3 17.6 %copy.31 = f32[16,256,1024]{1,0,2:T(8,128)} copy(f32[16,256,1024]{2,1,0:T(8,128)} %param.8) | data formatting | bytes 33554432 | tf_op args[0]
  54.9 12.5 %copy.30 = bf16[16,256,1024]{1,0,2:T(8,128)(2,1)} copy(bf16[16,256,1024]{2,1,0:T(8,128)(2,1)} %param.9) | data formatting | bytes 16777216 | tf_op args[1]
  67.4 11.1 %abs_reduce_fusion.1 = f32[16,1024]{0,1:T(8,128)} fusion(f32[16,256,1024]{1,0,2:T(8,128)} %copy.34, bf16[16,256,1024]{1,0,2:T(8,128)(2,1)} %copy.33), kind=kLoop, calls=%fused_computation.4 | loop fusion | flops 16760832 | bytes 25231360 | tf_op jit(solution)/shard_map/reduce_max | solution.py:23
  78.5 2.1 copy-done
  80.6 2.4 copy-done.1
  83.0 4.3 abs_reduce_fusion.2
  87.3 29.3 %abs_reduce_fusion = f32[16,1024]{0,1:T(8,128)} fusion(f32[16,1024,256]{2,1,0:T(8,128)} %param.12, bf16[16,1024,256]{2,1,0:T(8,128)(2,1)S(1)} %bitcast.14), kind=kLoop, calls=%fused_computation.2 | loop fusion | flops 16760832 | bytes 25231360 | tf_op jit(solution)/shard_map/reduce_max | solution.py:24
  116.6 92.5 %all-reduce.3.cloned.1.call-done = (f32[16,1024]{0,1:T(8,128)}, f32[16,1024]{0,1:T(8,128)}, f32[16,1024]{0,1:T(8,128)}) async-done(((f32[16,1024]{0,1:T(8,128)}, f32[16,1024]{0,1:T(8,128)}, f32[16,1024]{0,1:T(8,128)}), (f32[16,1024]{0,1:T(8,128)}, f32[16,1024]{0,1:T(8,128)}, f32[16,1024]{0,1:T(8,128)})) %all-reduce.3.cloned.1.call-update) | async-done | bytes 196624 | tf_op jit(solution)/shard_map/pmax | solution.py:20
  209.0 20.5 %divide_convert_fusion.1 = (bf16[16,256,1024]{1,0,2:T(8,128)(2,1)}, bf16[16,256,1024]{1,0,2:T(8,128)(2,1)S(1)}) fusion(f32[16,256,1024]{1,0,2:T(8,128)} %copy.34, bf16[16,256,1024]{1,0,2:T(8,128)(2,1)} %copy.33, f32[16,1024]{0,1:T(8,128)} %get-tuple-element.15, f32[16,1024]{0,1:T(8,128)} %get-tuple-element.14, f32[16,256,1024]{1,0,2:T(8,128)} %copy.31, ...), kind=kLoop, calls=%fused_computation.3 | loop fusion | flops 33554432 | bytes 67239936 | tf_op jit(solution)/shard_map/convert_element_type | solution.py:30
  229.6 187.0 %all_to_all.54 = bf16[16,256,1024]{1,0,2:T(8,128)(2,1)} all-to-all(bf16[16,256,1024]{1,0,2:T(8,128)(2,1)S(1)} %get-tuple-element.18), channel_id=1, replica_groups=mesh['expert'=4,'shard'=8] {'shard'}, dimensions={2} | all-to-all | bytes 16777216 | tf_op jit(solution)/shard_map/all_to_all | solution.py:34
  416.6 4.9 all-to-all-start.1
  421.5 23.8 %divide_convert_fusion = bf16[16,1024,256]{2,0,1:T(8,128)(2,1)} fusion(f32[16,1024,256]{2,1,0:T(8,128)} %param.12, f32[16,1024]{0,1:T(8,128)S(1)} %copy-done.2, bf16[16,1024,256]{2,1,0:T(8,128)(2,1)} %param.13), kind=kLoop, calls=%fused_computation.1 | loop fusion | flops 16777216 | bytes 33619968 | tf_op jit(solution)/shard_map/convert_element_type | solution.py:31
  445.3 158.3 %all-to-all-done.1 = bf16[16,256,1024]{1,0,2:T(8,128)(2,1)} async-done(((bf16[16,256,1024]{1,0,2:T(8,128)(2,1)}), bf16[16,256,1024]{1,0,2:T(8,128)(2,1)}, u32[]{:S(2)}, u32[]{:S(2)}) %all-to-all-start.1) | async-done | bytes 8388640 | tf_op jit(solution)/shard_map/all_to_all | solution.py:35
  603.6 5.0 all-to-all-start.2
  608.7 201.9 %all_gather.6 = bf16[2048,16]{0,1:T(8,128)(2,1)S(1)} all-gather(bf16[256,16]{0,1:T(8,128)(2,1)S(1)} %multiply_convert_fusion), channel_id=1, replica_groups=mesh['expert'=4,'shard'=8] {'shard'}, dimensions={0}, use_global_device_ids=true | all-gather | bytes 73728 | tf_op jit(solution)/shard_map/all_gather | solution.py:48
  810.6 6.0 all_gather.7
  816.5 0.8 constant_dynamic-slice_fusion
  818.7 0.8 constant_dynamic-slice_fusion.2
  820.2 12.3 %copy.32 = bf16[16,8,256,128]{3,2,1,0:T(8,128)(2,1)} copy(bf16[16,8,256,128]{2,0,3,1:T(8,128)(2,1)} %bitcast.15) | data formatting | bytes 16777216 | tf_op jit(solution)/shard_map/all_to_all | solution.py:34
  832.5 12.3 %copy.35 = bf16[16,8,256,128]{3,2,1,0:T(8,128)(2,1)} copy(bf16[16,8,256,128]{2,0,3,1:T(8,128)(2,1)} %bitcast.4) | data formatting | bytes 16777216 | tf_op jit(solution)/shard_map/all_to_all | solution.py:35
  844.8 11.4 %copy.38 = bf16[16,128,8,256]{3,2,1,0:T(8,128)(2,1)} copy(bf16[16,128,8,256]{3,0,1,2:T(8,128)(2,1)} %bitcast.7) | data formatting | bytes 16777216 | tf_op jit(solution)/shard_map/all_to_all | solution.py:37
  856.2 13.4 %all_to_all.50 = bf16[16,128,2048]{2,1,0:T(8,128)(2,1)} reshape(bf16[16,128,8,256]{3,2,1,0:T(8,128)(2,1)} %copy.38) | data formatting | bytes 16777216 | tf_op jit(solution)/shard_map/all_to_all | solution.py:37
  (21 shorter events, 2.8 us)
Async XLA Ops:
  7.2 201.8 %all-reduce.3.cloned.1.call-start = ((), (), s32[]{:S(2)}) async-start(), calls=%async_computation.3 | async-start | bytes 3145728 | tf_op jit(solution)/shard_map/pmax | solution.py:20
  67.4 13.2 %copy-start = (f32[16,256,1024]{1,0,2:T(8,128)S(1)}, f32[16,256,1024]{1,0,2:T(8,128)}, u32[]{:S(2)}) copy-start(f32[16,256,1024]{1,0,2:T(8,128)} %copy.31) | copy-start | bytes 50331652
  67.4 15.6 %copy-start.1 = (bf16[16,256,1024]{1,0,2:T(8,128)(2,1)S(1)}, bf16[16,256,1024]{1,0,2:T(8,128)(2,1)}, u32[]{:S(2)}) copy-start(bf16[16,256,1024]{1,0,2:T(8,128)(2,1)} %copy.30) | copy-start | bytes 25165828
  67.4 19.9 %slice-start = ((s8[8388608]{0:T(1024)(128)(4,1)}), s8[4194304]{0:T(1024)(128)(4,1)S(1)}, s32[]{:S(2)}) async-start(s8[8388608]{0:T(1024)(128)(4,1)} %bitcast.13), calls=%async_computation.4 | async-start | bytes 8388608
  83.0 4.3 slice-start.1
  229.6 192.0 %copy-start.2 = (f32[16,1024]{0,1:T(8,128)S(1)}, f32[16,1024]{0,1:T(8,128)}, u32[]{:S(2)}) copy-start(f32[16,1024]{0,1:T(8,128)} %get-tuple-element.16) | copy-start | bytes 196612
  416.6 187.0 %all-to-all-start.1 = ((bf16[16,256,1024]{1,0,2:T(8,128)(2,1)}), bf16[16,256,1024]{1,0,2:T(8,128)(2,1)}, u32[]{:S(2)}, u32[]{:S(2)}) async-start(bf16[16,256,1024]{1,0,2:T(8,128)(2,1)} %get-tuple-element.17), calls=%async_computation.1 | async-start | bytes 16777216 | tf_op jit(solution)/shard_map/all_to_all | solution.py:35
  445.3 163.3 %copy-start.3 = (f32[256,16]{0,1:T(8,128)S(1)}, f32[256,16]{0,1:T(8,128)}, u32[]{:S(2)}) copy-start(f32[256,16]{0,1:T(8,128)} %param.14) | copy-start | bytes 49156
  445.3 163.3 %copy-start.4 = (f32[256]{0:T(256)S(1)}, f32[256]{0:T(256)}, u32[]{:S(2)}) copy-start(f32[256]{0:T(256)} %param.15) | copy-start | bytes 3076
  603.6 241.2 %all-to-all-start.2 = ((bf16[16,1024,256]{2,0,1:T(8,128)(2,1)}), bf16[16,1024,256]{2,0,1:T(8,128)(2,1)}, u32[]{:S(2)}, u32[]{:S(2)}) async-start(bf16[16,1024,256]{2,0,1:T(8,128)(2,1)} %divide_convert_fusion), calls=%async_computation.2 | async-start | bytes 16777216 | tf_op jit(solution)/shard_map/all_to_all | solution.py:37
Sparse Core Ops, SparseCore 0:
  116.7 92.2 all-reduce.2
where the time goes:
time: 880 us; the launch traced here: 877 us
  blocking collectives  395 us (45%)
  waiting for transfers between devices  251 us (29%)
  local copies, waits for them, and re-layouts  118 us (13%)
  other arithmetic  88.9 us (10%)
  between operations  14.1 us (2%)
  starting transfers between devices  10 us (1%)
    all_gather x1, blocking collectives, per_device(): row_router = lax.all_gather(part_router, 'shard', axis=0, tiled=True)  202 us
    all_to_all x1, blocking collectives, per_device(): lax.all_to_all(narrow_gate, 'shard', split_axis=2, concat_axis=1, tiled=T...  187 us
    all_to_all x1, waiting for transfers between devices, per_device(): lax.all_to_all(narrow_up, 'shard', split_axis=2, concat_axis=1, tiled=True)  158 us
    pmax x1, waiting for transfers between devices, per_device(): lax.pmax((jnp.max(jnp.abs(merged_gate), axis=1), jnp.max(jnp.abs(merged_u...  92.5 us
    unnamed x22, local copies, waits for them, and re-layouts  67.4 us
    reduce_max x1, other arithmetic, per_device(): jnp.max(jnp.abs(merged_down), axis=2)  29.3 us
    all_to_all x2, local copies, waits for them, and re-layouts, per_device(): lax.all_to_all(narrow_down, 'shard', split_axis=1, concat_axis=2, tiled=T...  24.8 us
    convert_element_type x1, other arithmetic, per_device(): (merged_down / jnp.expand_dims(scale_down, 2)).astype(jnp.bfloat16)  23.8 us
  transfers between devices with their start and end apart: 3, of which 2 were waited for; matrix products, arithmetic and copies ran while one was open for 6% of the time, Pallas kernels for 0%

commit v1 on v0

--- a/solution.py
+++ b/solution.py
@@ -1,10 +1,273 @@
+import functools
+
 import jax
 import jax.numpy as jnp
 from jax import lax
+from jax.experimental import pallas as pl
+from jax.experimental.pallas import tpu as pltpu
 from jax.sharding import PartitionSpec as P
 
-
-def per_device(
+AHEAD = 2
+LAG_REDUCE = 4
+LAG_SCALE = 4
+LAG = LAG_REDUCE + LAG_SCALE
+HELD = AHEAD + LAG + 1
+QUEUED = 4
+LANES = 128
+
+
+def local_wait(ref, sem):
+    pltpu.make_async_copy(ref, ref, sem).wait()
+
+
+def kernel(
+    shards,
+    groups,
+    mg,
+    sg,
+    mu,
+    su,
+    md,
+    sd,
+    router,
+    out_g,
+    out_u,
+    out_d,
+    scale_g,
+    scale_u,
+    scale_d,
+    out_r,
+    wide,
+    wide_add,
+    wide_out,
+    tall,
+    tall_add,
+    tall_out,
+    part_max,
+    all_max,
+    scales,
+    load_sem,
+    add_sem,
+    max_send,
+    max_recv,
+    scale_send,
+    scale_recv,
+    data_send,
+    own_sem,
+    data_recv,
+    router_sem,
+):
+    experts, rows, cols = mg.shape
+    piece = cols // shards
+    chunks = 3 * experts
+    me = lax.axis_index("shard")
+    group = lax.axis_index("expert")
+    others = [lax.rem(me + k, shards) for k in range(1, shards)]
+
+    def remote(src, dst, send, recv, to):
+        return pltpu.make_async_remote_copy(
+            src_ref=src,
+            dst_ref=dst,
+            send_sem=send,
+            recv_sem=recv,
+            device_id=to,
+            device_id_type=pl.DeviceIdType.MESH,
+        )
+
+    def between(c, body):
+        pl.when(jnp.logical_and(c >= 0, c < chunks))(body)
+
+    def loads(c):
+        t, e = lax.div(c, experts), lax.rem(c, experts)
+        held, near = lax.rem(c, HELD), lax.rem(c, AHEAD + 1)
+        for k, (m, s, buf, add) in enumerate(
+            ((mg, sg, wide, wide_add), (mu, su, wide, wide_add), (md, sd, tall, tall_add))
+        ):
+
+            @pl.when(t == k)
+            def _():
+                pltpu.make_async_copy(m.at[e], buf.at[held], load_sem.at[near]).start()
+                pltpu.make_async_copy(s.at[e], add.at[near], add_sem.at[near]).start()
+
+    def merge(c):
+        t = lax.div(c, experts)
+        held, near = lax.rem(c, HELD), lax.rem(c, AHEAD + 1)
+
+        @pl.when(t < 2)
+        def _():
+            local_wait(wide.at[held], load_sem.at[near])
+            local_wait(wide_add.at[near], add_sem.at[near])
+            step = 32
+
+            def body(r, best):
+                at = pl.ds(pl.multiple_of(r * step, step), step)
+                x = wide[held, at, :] + wide_add[near, at, :].astype(jnp.float32)
+                wide[held, at, :] = x
+                return jnp.maximum(best, jnp.max(jnp.abs(x).reshape(step // 8, 8, cols), axis=0))
+
+            best = lax.fori_loop(0, rows // step, body, jnp.zeros((8, cols), jnp.float32))
+            best = jnp.max(best, axis=0, keepdims=True)
+            for d in range(shards):
+                part_max[c, d, :, :piece] = best[:, d * piece : (d + 1) * piece]
+
+        @pl.when(t == 2)
+        def _():
+            local_wait(tall.at[held], load_sem.at[near])
+            local_wait(tall_add.at[near], add_sem.at[near])
+
+            def body(d, carry):
+                at = pl.ds(pl.multiple_of(d * piece, piece), piece)
+                x = tall[held, at, :] + tall_add[near, at, :].astype(jnp.float32)
+                tall[held, at, :] = x
+                x = jnp.abs(x)
+                best = x[:, :LANES]
+                for k in range(1, rows // LANES):
+                    best = jnp.maximum(best, x[:, k * LANES : (k + 1) * LANES])
+                part_max[c, d, :, :piece] = jnp.max(best.T, axis=0, keepdims=True)
+                return carry
+
+            lax.fori_loop(0, shards, body, 0)
+
+        all_max[c, me] = part_max[c, me]
+
+    def send_max(c):
+        for d in others:
+            remote(
+                part_max.at[c, d], all_max.at[c, me], max_send, max_recv.at[c], {"shard": d}
+            ).start()
+
+    def reduce(c):
+        t, e = lax.div(c, experts), lax.rem(c, experts)
+        local_wait(all_max.at[c, pl.ds(0, shards - 1)], max_recv.at[c])
+        best = jnp.max(all_max[c], axis=0)
+        scales[c, me] = best
+        for k, ref in enumerate((scale_g, scale_u, scale_d)):
+
+            @pl.when(t == k)
+            def _():
+                ref[pl.ds(e, 1), :] = best[:, :piece]
+
+    def send_scale(c):
+        for d in others:
+            remote(
+                scales.at[c, me], scales.at[c, me], scale_send, scale_recv.at[c], {"shard": d}
+            ).start()
+
+    def narrow(c):
+        t = lax.div(c, experts)
+        held, queued = lax.rem(c, HELD), lax.rem(c, QUEUED)
+        local_wait(scales.at[c, pl.ds(0, shards - 1)], scale_recv.at[c])
+
+        @pl.when(t < 2)
+        def _():
+            for d in range(shards):
+                inverse = 1.0 / scales[c, d, :, :piece]
+                x = wide[held, :, d * piece : (d + 1) * piece]
+                wide_out[queued, d] = (x * inverse).astype(jnp.bfloat16)
+
+        @pl.when(t == 2)
+        def _():
+            def body(d, carry):
+                at = pl.ds(pl.multiple_of(d * piece, piece), piece)
+                inverse = 1.0 / scales[c, d, :, :piece]
+                inverse = jnp.broadcast_to(inverse, (LANES, piece)).T
+                for k in range(rows // LANES):
+                    lanes = slice(k * LANES, (k + 1) * LANES)
+                    tall_out[queued, d, :, lanes] = (tall[held, at, lanes] * inverse).astype(
+                        jnp.bfloat16
+                    )
+                return carry
+
+            lax.fori_loop(0, shards, body, 0)
+
+    mine = pl.ds(pl.multiple_of(me * rows, rows), rows)
+
+    def send_data(c):
+        t, e = lax.div(c, experts), lax.rem(c, experts)
+        queued = lax.rem(c, QUEUED)
+        for k, (src, dst) in enumerate(
+            (
+                (wide_out, out_g.at[e, mine, :]),
+                (wide_out, out_u.at[e, mine, :]),
+                (tall_out, out_d.at[e, :, mine]),
+            )
+        ):
+
+            @pl.when(t == k)
+            def _():
+                for d in others:
+                    remote(
+                        src.at[queued, d],
+                        dst,
+                        data_send.at[queued],
+                        data_recv.at[k],
+                        {"shard": d},
+                    ).start()
+                pltpu.make_async_copy(src.at[queued, me], dst, own_sem.at[queued]).start()
+
+    def sent_data(c):
+        t = lax.div(c, experts)
+        queued = lax.rem(c, QUEUED)
+        for kind, src in ((t < 2, wide_out), (t == 2, tall_out)):
+
+            @pl.when(kind)
+            def _():
+                local_wait(src.at[queued, pl.ds(0, shards - 1)], data_send.at[queued])
+                local_wait(src.at[queued, 0], own_sem.at[queued])
+
+    wide_r = router.shape[0]
+    my_experts = pl.ds(pl.multiple_of(group * wide_r, wide_r), wide_r)
+
+    def router_rows():
+        at = out_r.at[my_experts, mine]
+        for d in others:
+            remote(router, at, router_sem.at[0], router_sem.at[1], {"shard": d}).start()
+        pltpu.make_async_copy(router, at, router_sem.at[2]).start()
+
+    def router_columns():
+        local_wait(router, router_sem.at[2])
+        gathered = out_r.at[my_experts, pl.ds(0, rows * (shards - 1))]
+        local_wait(gathered, router_sem.at[1])
+        for k in range(1, groups):
+            to = lax.rem(group + k, groups)
+            remote(
+                out_r.at[my_experts],
+                out_r.at[my_experts],
+                router_sem.at[3],
+                router_sem.at[4],
+                {"expert": to},
+            ).start()
+
+    def step(i, carry):
+        between(i + AHEAD, lambda: loads(i + AHEAD))
+        between(i - LAG_REDUCE, lambda: reduce(i - LAG_REDUCE))
+        between(i, lambda: merge(i))
+        between(i - LAG_REDUCE, lambda: send_scale(i - LAG_REDUCE))
+        between(i, lambda: send_max(i))
+        between(i - LAG - 1, lambda: send_data(i - LAG - 1))
+        pl.when(i == chunks // 2)(router_rows)
+        pl.when(i == chunks)(router_columns)
+        between(i - LAG - QUEUED, lambda: sent_data(i - LAG - QUEUED))
+        between(i - LAG, lambda: narrow(i - LAG))
+        return carry
+
+    for c in range(AHEAD):
+        loads(jnp.int32(c))
+    lax.fori_loop(0, chunks + LAG + QUEUED, step, 0)
+
+    for k, out in enumerate((out_g, out_u)):
+        local_wait(out.at[:, pl.ds(0, rows * (shards - 1)), :], data_recv.at[k])
+    local_wait(out_d.at[:, :, pl.ds(0, rows * (shards - 1))], data_recv.at[2])
+    local_wait(part_max.at[:, pl.ds(0, shards - 1)], max_send)
+    local_wait(scales.at[:, pl.ds(0, shards - 1)], scale_send)
+    local_wait(out_r.at[my_experts, pl.ds(0, rows * (shards - 1))], router_sem.at[0])
+    if groups > 1:
+        rest = out_r.at[pl.ds(0, wide_r * (groups - 1))]
+        local_wait(rest, router_sem.at[3])
+        local_wait(rest, router_sem.at[4])
+
+
+def by_collectives(
     master_gate,
     second_gate,
     master_up,
@@ -50,6 +313,79 @@
     return (final_gate, final_up, final_down, scale_gate, scale_up, scale_down, serve_router)
 
 
+def per_device(
+    shards,
+    groups,
+    master_gate,
+    second_gate,
+    master_up,
+    second_up,
+    master_down,
+    second_down,
+    router_weight,
+    router_gain,
+):
+    experts, rows, cols = master_gate.shape
+    piece = cols // shards
+    chunks = 3 * experts
+    if piece % LANES or rows % LANES:
+        return by_collectives(
+            master_gate,
+            second_gate,
+            master_up,
+            second_up,
+            master_down,
+            second_down,
+            router_weight,
+            router_gain,
+        )
+    router = (router_weight * router_gain[:, None]).astype(jnp.bfloat16).T
+    anywhere = pl.BlockSpec(memory_space=pl.ANY)
+    vmem = pl.BlockSpec(memory_space=pltpu.VMEM)
+    f32, bf16, dma = jnp.float32, jnp.bfloat16, pltpu.SemaphoreType.DMA
+    shape = jax.ShapeDtypeStruct
+    small = max(piece, LANES)
+    *outs, served = pl.pallas_call(
+        functools.partial(kernel, shards, groups),
+        out_shape=(
+            shape((experts, rows * shards, piece), bf16),
+            shape((experts, rows * shards, piece), bf16),
+            shape((experts, piece, rows * shards), bf16),
+            shape((experts, piece), f32),
+            shape((experts, piece), f32),
+            shape((experts, piece), f32),
+            shape((router.shape[0] * groups, rows * shards), bf16),
+        ),
+        in_specs=[anywhere] * 6 + [vmem],
+        out_specs=(anywhere, anywhere, anywhere, vmem, vmem, vmem, anywhere),
+        scratch_shapes=[
+            pltpu.VMEM((HELD, rows, cols), f32),
+            pltpu.VMEM((AHEAD + 1, rows, cols), bf16),
+            pltpu.VMEM((QUEUED, shards, rows, piece), bf16),
+            pltpu.VMEM((HELD, cols, rows), f32),
+            pltpu.VMEM((AHEAD + 1, cols, rows), bf16),
+            pltpu.VMEM((QUEUED, shards, piece, rows), bf16),
+            pltpu.VMEM((chunks, shards, 1, small), f32),
+            pltpu.VMEM((chunks, shards, 1, small), f32),
+            pltpu.VMEM((chunks, shards, 1, small), f32),
+            dma((AHEAD + 1,)),
+            dma((AHEAD + 1,)),
+            dma,
+            dma((chunks,)),
+            dma,
+            dma((chunks,)),
+            dma((QUEUED,)),
+            dma((QUEUED,)),
+            dma((3,)),
+            dma((5,)),
+        ],
+        compiler_params=pltpu.CompilerParams(
+            has_side_effects=True, vmem_limit_bytes=60 * 1024 * 1024
+        ),
+    )(master_gate, second_gate, master_up, second_up, master_down, second_down, router)
+    return (*outs, served.T)
+
+
 def solution(mesh):
     in_specs = (
         P("expert", "shard", None),
@@ -71,5 +407,9 @@
         P(),
     )
     return jax.shard_map(
-        per_device, mesh=mesh, in_specs=in_specs, out_specs=out_specs, check_vma=False
-    )
+        functools.partial(per_device, mesh.shape["shard"], mesh.shape["expert"]),
+        mesh=mesh,
+        in_specs=in_specs,
+        out_specs=out_specs,
+        check_vma=False,
+    )

time: 880 us -> 597 us (0.68)
  Pallas kernels: 0 us -> 568 us
  blocking collectives: 395 us -> 0 us
  waiting for transfers between devices: 251 us -> 0 us
  local copies, waits for them, and re-layouts: 118 us -> 26.2 us
  other arithmetic: 88.9 us -> 1.32 us
  between operations: 14.1 us -> 0.65 us
  starting transfers between devices: 10 us -> 0 us
    pallas_call x0 -> x1, Pallas kernels: none -> 568 us  [per_device(): pl.pallas_call(functools.partial(kernel, shards, groups), out_shape=(shap...]
    all_gather x2 -> x0, blocking collectives: 208 us -> none  [the longest x1 202 us: per_device(): row_router = lax.all_gather(part_router, 'shard', axis=0, tiled=True)]
    all_to_all x1 -> x0, blocking collectives: 187 us -> none  [per_device(): lax.all_to_all(narrow_gate, 'shard', split_axis=2, concat_axis=1, tiled=T...]
    all_to_all x2 -> x0, waiting for transfers between devices: 158 us -> none  [the longest x1 158 us: per_device(): lax.all_to_all(narrow_up, 'shard', split_axis=2, concat_axis=1, tiled=True)]
    pmax x1 -> x0, waiting for transfers between devices: 92.5 us -> none  [per_device(): lax.pmax((jnp.max(jnp.abs(merged_gate), axis=1), jnp.max(jnp.abs(merged_u...]
    all_to_all x4 -> x0, local copies, waits for them, and re-layouts: 49.4 us -> none  [the longest x2 24.8 us: per_device(): lax.all_to_all(narrow_down, 'shard', split_axis=1, concat_axis=2, tiled=T...]
    reduce_max x3 -> x0, other arithmetic: 44.6 us -> none  [the longest x1 29.3 us: per_device(): jnp.max(jnp.abs(merged_down), axis=2)]
    convert_element_type x3 -> x0, other arithmetic: 44.3 us -> none  [the longest x1 23.8 us: per_device(): (merged_down / jnp.expand_dims(scale_down, 2)).astype(jnp.bfloat16)]
  transfers between devices with their start and end apart: 3 -> 0, of which waited for: 2 -> 0; matrix products, arithmetic and copies ran while one was open for 6% -> 0% of each run, Pallas kernels for 0% -> 0%
where the time goes in v1:
time: 597 us; the launch traced here: 596 us
  Pallas kernels  568 us (95%)
  local copies, waits for them, and re-layouts  26.2 us (4%)
    pallas_call x1, Pallas kernels, per_device(): pl.pallas_call(functools.partial(kernel, shards, groups), out_shape=(shap...  568 us
    unnamed x15, local copies, waits for them, and re-layouts  26.2 us

profile of v1, /device:TPU:0, one launch (start us, length us, event | category | flops | bytes accessed | tf_op | source)
XLA Modules:
  0.0 596.1 jit_solution(6409745527112013555)
XLA Ops:
  0.6 1.3 fusion.router
  2.0 567.9 %shard_map.135 = (bf16[16,2048,128]{2,1,0:T(8,128)(2,1)}, bf16[16,2048,128]{2,1,0:T(8,128)(2,1)}, bf16[16,128,2048]{2,1,0:T(8,128)(2,1)}, f32[16,128]{1,0:T(8,12...) custom-call(f32[16,256,1024]{2,1,0:T(8,128)} %mg.1, bf16[16,256,1024]{2,1,0:T(8,128)(2,1)} %sg.1, ...), custom_call_target="tpu_custom_call" | custom-call | tf_op jit(solution)/shard_map/pallas_call | solution.py:348
  569.9 7.6 %copy.22 = bf16[16,2048,128]{2,1,0:T(8,128)(2,1)} copy(bf16[16,2048,128]{2,1,0:T(8,128)(2,1)} %get-tuple-element.28) | data formatting | bytes 16777216
  577.5 7.6 %copy.23 = bf16[16,2048,128]{2,1,0:T(8,128)(2,1)} copy(bf16[16,2048,128]{2,1,0:T(8,128)(2,1)} %get-tuple-element.29) | data formatting | bytes 16777216
  585.1 0.0 copy-start.3
  585.1 0.0 copy-start.2
  585.1 0.0 copy-start.1
  585.1 0.0 copy-start
  585.1 8.5 %copy.24 = bf16[16,128,2048]{2,1,0:T(8,128)(2,1)} copy(bf16[16,128,2048]{2,1,0:T(8,128)(2,1)} %get-tuple-element.30) | data formatting | bytes 16777216
  593.6 0.0 copy-done.3
  593.6 0.6 copy.25
  594.2 0.0 copy-done.2
  594.2 0.6 copy.26
  594.8 0.0 copy-done.1
  594.8 0.6 copy.27
  595.4 0.0 copy-done
  595.4 0.7 copy.28
Async XLA Ops:
  585.1 8.5 %copy-start.3 = (f32[16,128]{1,0:T(8,128)S(1)}, f32[16,128]{1,0:T(8,128)}, u32[]{:S(2)}) copy-start(f32[16,128]{1,0:T(8,128)} %get-tuple-element.31) | copy-start | bytes 24580
  585.1 9.1 %copy-start.2 = (f32[16,128]{1,0:T(8,128)S(1)}, f32[16,128]{1,0:T(8,128)}, u32[]{:S(2)}) copy-start(f32[16,128]{1,0:T(8,128)} %get-tuple-element.32) | copy-start | bytes 24580
  585.1 9.7 %copy-start.1 = (f32[16,128]{1,0:T(8,128)S(1)}, f32[16,128]{1,0:T(8,128)}, u32[]{:S(2)}) copy-start(f32[16,128]{1,0:T(8,128)} %get-tuple-element.33) | copy-start | bytes 24580
  585.1 10.3 %copy-start = (bf16[64,2048]{1,0:T(8,128)(2,1)S(1)}, bf16[64,2048]{1,0:T(8,128)(2,1)}, u32[]{:S(2)}) copy-start(bf16[64,2048]{1,0:T(8,128)(2,1)} %get-tuple-element.20) | copy-start | bytes 786436
